TPU v7x, 256 devices: a whole 4x4x8 slice. The times are simulated.
256 devices in a mesh: fsdp: 32 (over x_lo, z, core), dp: 8 (over y, x_hi).
Axes of the slice: x: 4 (x_hi: 2, x_lo: 2; x = x_hi * 2 + x_lo), y: 4, z: 8, core: 2. Of those that a mesh axis runs over, the one named last changes fastest.
Arguments:
- inputs: bfloat16 [49152, 4096], P(('fsdp', 'dp')), may hold values from -6 to 6
- grad_out: bfloat16 [49152, 14336], P(('fsdp', 'dp')), may hold values from -0.0068359375 to 0.0068359375
- projection: bfloat16 [4096, 128], P('fsdp'), may hold values from -0.375 to 0.375
- moment: float32 [14336, 128], P('fsdp'), may hold values from -1.5 to 1.5
- second: float32 [14336, 128], P('fsdp'), may hold values from 0.0001 to 0.001
Outputs:
- update: bfloat16 [4096, 14336], P('fsdp')
- new_moment: float32 [14336, 128], P('fsdp')
- new_second: float32 [14336, 128], P('fsdp')
All inputs are finite; a program needn't handle non-finite values.
Results may differ from a plain program's by a relative error of at most 0.0051.
Values may be sent and summed in bfloat16 or wider, within the bound.
A program may use at most 64 MiB of HBM per device.

v0:
```python
import jax
import jax.numpy as jnp
from jax import lax
from jax.sharding import Mesh
from jax.sharding import PartitionSpec as P

STEP = 10
FSDP = ("fsdp_0", "fsdp_1", "fsdp_2")
FSDP_DP = ("fsdp_0", "fsdp_1", "fsdp_2", "dp")


def copy_for_each(x, axis):
    copies = jnp.broadcast_to(x, (lax.axis_size(axis), *x.shape))
    return lax.all_to_all(copies, axis, split_axis=0, concat_axis=0, tiled=True)


def in_order(parts, dim):
    shape = list(parts.shape[1:])
    shape[dim] *= parts.shape[0]
    return jnp.moveaxis(parts, 0, dim).reshape(shape)


def collect(x, axis, dim):
    parts = copy_for_each(x, axis)
    return in_order(parts, dim)


def split_up(x, dim, peers):
    before, after = (x.shape[:dim], x.shape[dim + 1 :])
    return jnp.moveaxis(x.reshape(*before, peers, -1, *after), dim, 0)


def scatter_pairs(x, chips, core, dim):
    sizes = (lax.axis_size(chips), lax.axis_size(core))
    parts = split_up(x, dim, sizes[0] * sizes[1])
    inside = parts.shape[1:]
    parts = parts.reshape(*sizes, *inside).swapaxes(0, 1).reshape(-1, *inside)
    parts = lax.psum_scatter(parts, core, scatter_dimension=0, tiled=True)
    return lax.psum_scatter(parts, chips, scatter_dimension=0, tiled=True)[0]


def of_everyone(x, axis):
    everything = copy_for_each(x, axis)
    return jnp.sum(everything, axis=0)


def adam_step(low_rank, moment, second):
    new_moment = 0.9 * moment + 0.1 * low_rank
    new_second = 0.999 * second + 0.001 * (low_rank * low_rank)
    first_fix = 1.0 - 0.9**STEP
    second_fix = 1.0 - 0.999**STEP
    normalized = (new_moment / first_fix / (jnp.sqrt(new_second / second_fix) + 1e-08)).astype(
        jnp.bfloat16
    )
    return (new_moment, new_second, normalized)


def local(inputs, grad_out, projection, moment, second):
    projected = jnp.dot(
        inputs, collect(projection, FSDP, 0), preferred_element_type=jnp.float32
    ).astype(jnp.bfloat16)
    contract = (((0,), (0,)), ((), ()))
    low_rank = scatter_pairs(
        lax.dot_general(grad_out, projected, contract, preferred_element_type=jnp.float32),
        ("fsdp_0", "fsdp_1"),
        "fsdp_2",
        0,
    )
    low_rank = of_everyone(low_rank, "dp")
    new_moment, new_second, normalized = adam_step(low_rank, moment, second)
    expand = (((1,), (1,)), ((), ()))
    update = lax.dot_general(
        projection,
        lax.all_gather(normalized, FSDP, axis=0, tiled=True),
        expand,
        preferred_element_type=jnp.float32,
    ).astype(jnp.bfloat16)
    return (update, new_moment, new_second)


def solution(mesh):
    split = Mesh(
        mesh.devices.reshape(2, 8, 2, mesh.shape["dp"]), ("fsdp_0", "fsdp_1", "fsdp_2", "dp")
    )
    return jax.shard_map(
        local,
        mesh=split,
        in_specs=(P(FSDP_DP, None), P(FSDP_DP, None), P(FSDP, None), P(FSDP, None), P(FSDP, None)),
        out_specs=(P(FSDP, None), P(FSDP, None), P(FSDP, None)),
        check_vma=False,
    )
```

profile of v0, /device:TPU:1, one launch (start us, length us, event | category | flops | bytes accessed | tf_op | source)
XLA Modules:
  0.0 277.3 jit_solution(1353939282653781149)
XLA Ops:
  7.2 0.0 copy-start
  7.2 0.0 reduce-scatter.3.cloned.1.call-start
  7.2 1.1 broadcast_in_dim.6
  8.3 37.4 %all_to_all.10 = bf16[32,128,128]{2,1,0:T(8,128)(2,1)S(1)} all-to-all(bf16[32,128,128]{2,1,0:T(8,128)(2,1)S(1)} %broadcast_in_dim.6), channel_id=1, replica_groups=mesh['fsdp_0'=2,'fsdp_1'=8,'fsdp_2'=2,'dp'=8] {'fsdp_0','fsdp_1','fsdp_2'}, dimensions={0} | all-to-all | bytes 2097152 | tf_op jit(solution)/shard_map/all_to_all | solution.py:14
  45.7 0.0 copy-done
  45.7 7.3 %convolution_bitcast_fusion = f32[14336,128]{0,1:T(8,128)} fusion(bf16[192,14336]{1,0:T(8,128)(2,1)} %param.6, bf16[192,4096]{1,0:T(8,128)(2,1)S(1)} %copy-done, bf16[4096,128]{1,0:T(8,128)(2,1)S(1)} %bitcast.17), kind=kOutput, calls=%fused_computation | convolution fusion | flops 905994240 | bytes 15466496 | tf_op jit(solution)/shard_map/dot_general | solution.py:64
  53.0 8.6 %copy.12 = f32[14336,128]{1,0:T(8,128)} copy(f32[14336,128]{0,1:T(8,128)} %convolution_bitcast_fusion) | data formatting | bytes 14680064 | tf_op jit(solution)/shard_map/dot_general | solution.py:64
  61.6 6.9 %copy.13 = f32[2,16,448,128]{3,2,1,0:T(8,128)} copy(f32[2,16,448,128]{3,2,0,1:T(8,128)} %bitcast.16) | data formatting | bytes 14680064 | tf_op jit(solution)/shard_map/transpose | solution.py:37
  68.5 0.0 reduce-scatter.3.cloned.1.call-update
  68.5 0.0 reduce-scatter.5.cloned.1.call-start
  68.6 21.3 %reduce-scatter.3.cloned.1.call-done = f32[16,448,128]{2,1,0:T(8,128)} async-done(((f32[32,448,128]{2,1,0:T(8,128)}), f32[16,448,128]{2,1,0:T(8,128)}) %reduce-scatter.3.cloned.1.call-update) | async-done | bytes 3670032 | tf_op jit(solution)/shard_map/reduce_scatter | solution.py:38
  89.8 0.0 reduce-scatter.5.cloned.1.call-update
  89.9 0.0 all-gather.2.cloned.1.call-start
  89.9 73.8 %reduce-scatter.5.cloned.1.call-done = f32[1,448,128]{2,1,0:T(8,128)} async-done(((f32[16,448,128]{2,1,0:T(8,128)}), f32[1,448,128]{2,1,0:T(8,128)}) %reduce-scatter.5.cloned.1.call-update) | async-done | bytes 229392 | tf_op jit(solution)/shard_map/reduce_scatter | solution.py:39
  163.7 1.1 broadcast_in_dim.7
  164.7 0.0 copy-start.1
  164.7 22.2 %all_to_all.11 = f32[8,448,128]{2,1,0:T(8,128)S(1)} all-to-all(f32[8,448,128]{2,1,0:T(8,128)S(1)} %broadcast_in_dim.7), channel_id=1, replica_groups=mesh['fsdp_0'=2,'fsdp_1'=8,'fsdp_2'=2,'dp'=8] {'dp'}, dimensions={0} | all-to-all | bytes 3670016 | tf_op jit(solution)/shard_map/all_to_all | solution.py:14
  186.9 0.8 reduce_sum.9
  187.7 2.0 divide_convert_fusion
  189.7 0.0 all-gather.2.cloned.1.call-update
  189.8 70.0 %all-gather.2.cloned.1.call-done = bf16[14336,128]{1,0:T(8,128)(2,1)} async-done(((bf16[448,128]{1,0:T(8,128)(2,1)}), bf16[14336,128]{1,0:T(8,128)(2,1)}) %all-gather.2.cloned.1.call-update) | async-done | bytes 3670032 | tf_op jit(solution)/shard_map/all_gather | solution.py:74
  259.7 0.0 copy-done.1
  259.7 5.0 %fusion = bf16[128,14336]{0,1:T(8,128)(2,1)} fusion(bf16[14336,128]{1,0:T(8,128)(2,1)} %all-gather.2.cloned.1.call-done, bf16[128,128]{1,0:T(8,128)(2,1)S(1)} %copy-done.1), kind=kOutput, calls=%fused_computation.2 | convolution fusion | flops 471597056 | bytes 7372800 | tf_op jit(solution)/shard_map/dot_general | solution.py:72
  264.7 6.1 %copy.14 = bf16[128,14336]{1,0:T(8,128)(2,1)} copy(bf16[128,14336]{0,1:T(8,128)(2,1)} %fusion) | data formatting | bytes 7340032
Async XLA Ops:
  7.2 38.5 %copy-start = (bf16[192,4096]{1,0:T(8,128)(2,1)S(1)}, bf16[192,4096]{1,0:T(8,128)(2,1)}, u32[]{:S(2)}) copy-start(bf16[192,4096]{1,0:T(8,128)(2,1)} %param.5) | copy-start | bytes 4718596
  7.2 82.7 %reduce-scatter.3.cloned.1.call-start = ((), (), s32[]{:S(2)}) async-start(), calls=%async_computation.4 | async-start | bytes 11010048 | tf_op jit(solution)/shard_map/reduce_scatter | solution.py:38
  68.5 95.1 %reduce-scatter.5.cloned.1.call-start = ((), (), s32[]{:S(2)}) async-start(), calls=%async_computation.5 | async-start | bytes 3899392 | tf_op jit(solution)/shard_map/reduce_scatter | solution.py:39
  89.9 169.9 %all-gather.2.cloned.1.call-start = ((), (), s32[]{:S(2)}) async-start(), calls=%async_computation.6 | async-start | bytes 3784704 | tf_op jit(solution)/shard_map/all_gather | solution.py:74
  164.7 95.0 %copy-start.1 = (bf16[128,128]{1,0:T(8,128)(2,1)S(1)}, bf16[128,128]{1,0:T(8,128)(2,1)}, u32[]{:S(2)}) copy-start(bf16[128,128]{1,0:T(8,128)(2,1)} %param.7) | copy-start | bytes 98308
Sparse Core Ops, SparseCore 0:
  68.6 21.1 reduce-scatter.2
  92.4 71.2 reduce-scatter.4
  189.9 69.7 all-gather.1
where the time goes:
time: 278 us; the launch traced here: 277 us
  waiting for transfers between devices  165 us (59%)
  blocking collectives  59.6 us (21%)
  local copies, waits for them, and re-layouts  23.8 us (9%)
  between operations  13.8 us (5%)
  matrix products  12.3 us (4%)
  other arithmetic  2.82 us (1%)
    reduce_scatter x1, waiting for transfers between devices, scatter_pairs(): return lax.psum_scatter(parts, chips, scatter_dimension=0, tiled=True)[0]  73.8 us
    all_gather x1, waiting for transfers between devices, local(): lax.all_gather(normalized, FSDP, axis=0, tiled=True)  70 us
    all_to_all x2, blocking collectives, copy_for_each(): return lax.all_to_all(copies, axis, split_axis=0, concat_axis=0, tiled=True)  59.6 us
    reduce_scatter x1, waiting for transfers between devices, scatter_pairs(): parts = lax.psum_scatter(parts, core, scatter_dimension=0, tiled=True)  21.3 us
    dot_general x1, local copies, waits for them, and re-layouts, local(): lax.dot_general(grad_out, projected, contract, preferred_element_type=jnp...  8.64 us
    dot_general x1, matrix products, local(): lax.dot_general(grad_out, projected, contract, preferred_element_type=jnp...  7.29 us
    transpose x1, local copies, waits for them, and re-layouts, scatter_pairs(): parts = parts.reshape(*sizes, *inside).swapaxes(0, 1).reshape(-1, *inside)  6.88 us
    unnamed x5, local copies, waits for them, and re-layouts  6.09 us
  transfers between devices with their start and end apart: 3, of which 3 were waited for; matrix products, arithmetic and copies ran while one was open for 0% of the time, Pallas kernels for 0%

commit v1 on v0

v1 whole, which is shorter than its diff:
```python
import jax
import jax.numpy as jnp
from jax import lax
from jax.experimental import pallas as pl
from jax.experimental.pallas import tpu as pltpu
from jax.sharding import Mesh
from jax.sharding import PartitionSpec as P

STEP = 10
AXES = ("xl", "z", "c", "y", "xh")
FSDP = ("xl", "z", "c")
MESH = pl.DeviceIdType.MESH
F32 = jnp.float32
BF16 = jnp.bfloat16


def adam(low_rank, moment, second):
    new_moment = 0.9 * moment + 0.1 * low_rank
    new_second = 0.999 * second + 0.001 * (low_rank * low_rank)
    return new_moment, new_second


def normalize(new_moment, new_second):
    first_fix = 1.0 - 0.9**STEP
    second_fix = 1.0 - 0.999**STEP
    return (new_moment / first_fix / (jnp.sqrt(new_second / second_fix) + 1e-08)).astype(BF16)


def comm_kernel(
    inputs, grad, proj, moment, second,
    full, lr_out,
    xk, pb, gb, part, pt, ms, t, fwd, own, fsum, u, fwd2, own2, fsum2, w, zr, lr_mine,
    sem_l, sem_x, sem_ps, sem_pr, sem_ts, sem_tr, sem_gs, sem_gr, sem_ms, sem_mr,
    sem_1s, sem_1r, sem_2s, sem_2r, sem_zs, sem_zr, sem_ls, sem_lr,
    sem_gzs, sem_gzr, sem_bs, sem_br, sem_as, sem_ar, sem_ds, sem_dr,
):
    xl, z, c, y, xh = (lax.axis_index(n) for n in AXES)
    x = 2 * xh + xl
    tok = inputs.shape[0]
    rank = proj.shape[1]
    piece = w.shape[2]
    half_cols = gb.shape[2]
    blk = 8 * piece
    other = 1 - c
    pa = x + c * (y - x)
    pb_ = y + c * (x - y)

    def at(xx, yy):
        return {"xl": lax.rem(xx, 2), "xh": lax.div(xx, 2), "y": yy}

    def a_dev(s):
        return at(lax.rem(x + s * (1 - c) + 4, 4), lax.rem(y + s * c + 4, 4))

    def b_dev(s):
        return at(lax.rem(x + s * c + 4, 4), lax.rem(y + s * (1 - c) + 4, 4))

    partner = {"c": other}
    mine_z = lax.div(z, 4) == c

    def remote(src, dst, ssem, rsem, dev):
        return pltpu.make_async_remote_copy(
            src_ref=src, dst_ref=dst, send_sem=ssem, recv_sem=rsem, device_id=dev, device_id_type=MESH
        )

    def cols(i, n):
        return pl.ds(pl.multiple_of(i, 128), n)

    def rows(i, n):
        return pl.ds(pl.multiple_of(i, 16), n)

    p_row = rows((xl * 8 + z) * rank, rank)
    p_load = pltpu.make_async_copy(proj, pb.at[p_row], sem_l.at[0])
    p_load.start()
    mine = rows(c * tok, tok)
    for j in range(16):
        pltpu.make_async_copy(
            inputs.at[:, cols((2 * j + c) * rank, rank)], xk.at[mine, pl.ds(j * rank, rank)], sem_l.at[1]
        ).start()
    for k in range(2):
        pltpu.make_async_copy(
            grad.at[:, cols(k * 2 * half_cols + c * half_cols, half_cols)], gb.at[k, mine], sem_l.at[2 + k]
        ).start()
    m_row = pl.ds(pl.multiple_of(y * piece, 8), piece)
    own_state = jnp.logical_and(mine_z, xh == c)
    gets_state = jnp.logical_and(mine_z, xh != c)
    gives_state = jnp.logical_and(jnp.logical_not(mine_z), xh == c)

    @pl.when(own_state)
    def _():
        pltpu.make_async_copy(moment.at[m_row], ms.at[0], sem_l.at[4]).start()
        pltpu.make_async_copy(second.at[m_row], ms.at[1], sem_l.at[5]).start()

    barrier = pltpu.get_barrier_semaphore()

    def greet(dev):
        pl.semaphore_signal(barrier, inc=1, device_id=dev, device_id_type=MESH)

    for d in range(1, 8):
        greet({"z": lax.rem(z + d, 8)})
    for s in (1, -1):
        greet(at(lax.rem(x + s + 4, 4), y))
    for dx in range(2):
        for dy in range(4):
            for dc in range(2):
                if dx or dy or dc:
                    greet({"xh": lax.rem(xh + dx, 2), "y": lax.rem(y + dy, 4), "c": lax.rem(c + dc, 2)})
    pl.semaphore_wait(barrier, 24)

    p_load.wait()
    sends = []
    for d in (4, 3, 5, 2, 6, 1, 7):
        cp = remote(pb.at[p_row], pb.at[p_row], sem_ps.at[d], sem_pr.at[d], {"z": lax.rem(z + d, 8)})
        cp.start()
        sends.append(cp)
    x_right = at(lax.rem(x + 1, 4), y)
    x_left = at(lax.rem(x + 3, 4), y)

    def forward(rel):
        row = rows((xl * 8 + lax.rem(z + rel, 8)) * rank, rank)
        cp = remote(pb.at[row], pb.at[row], sem_ps.at[8 + rel], sem_pr.at[8 + rel], x_right if rel < 4 else x_left)
        cp.start()
        sends.append(cp)

    forward(0)
    theirs = rows(other * tok, tok)
    for j in range(16):
        remote(
            inputs.at[:, cols((2 * j + other) * rank, rank)], xk.at[mine, pl.ds(j * rank, rank)],
            sem_x.at[0], sem_x.at[1], partner,
        ).start()
    x_swap = remote(xk.at[mine], xk.at[theirs], sem_x.at[0], sem_x.at[1], partner)
    for k in range(2):
        cp = remote(
            grad.at[:, cols(k * 2 * half_cols + other * half_cols, half_cols)], gb.at[k, mine],
            sem_gs.at[k], sem_gr.at[k], partner,
        )
        cp.start()
        sends.append(cp)

    @pl.when(gives_state)
    def _():
        remote(moment.at[m_row], ms.at[0], sem_ms.at[0], sem_mr.at[0], partner).start()
        remote(second.at[m_row], ms.at[1], sem_ms.at[1], sem_mr.at[1], partner).start()

    for d in (1, 7, 2, 6, 3, 5, 4):
        row = rows((xl * 8 + lax.rem(z + 8 - d, 8)) * rank, rank)
        remote(pb.at[row], pb.at[row], sem_ps.at[d], sem_pr.at[d], x_right).wait_recv()
        forward(8 - d)
    for rel in range(8):
        row = rows(((1 - xl) * 8 + lax.rem(z + rel, 8)) * rank, rank)
        remote(pb.at[row], pb.at[row], sem_ps.at[8 + rel], sem_pr.at[8 + rel], x_right).wait_recv()

    pltpu.make_async_copy(xk.at[mine], xk.at[mine], sem_l.at[1]).wait()
    x_swap.wait()
    part[0] = jnp.dot(xk[...], pb[...], preferred_element_type=F32)
    p_swap = remote(part.at[0], part.at[1], sem_ts.at[0], sem_tr.at[0], partner)
    p_swap.start()
    p_swap.wait()
    pt[...] = (part[0] + part[1]).T.astype(BF16)

    for k in range(2):
        pltpu.make_async_copy(gb.at[k, mine], gb.at[k, mine], sem_l.at[2 + k]).wait()
        remote(gb.at[k, theirs], gb.at[k, theirs], sem_gs.at[k], sem_gr.at[k], partner).wait_recv()
    right, left, opp = lax.rem(pa + 1, 4), lax.rem(pa + 3, 4), lax.rem(pa + 2, 4)
    dev_r, dev_l = a_dev(1), a_dev(-1)

    def compute_half(h):
        def body(i, carry):
            zl, k = lax.div(i, 2), lax.rem(i, 2)
            g = gb[k, :, cols((2 * h + zl) * blk, blk)]
            out = lax.dot_general(pt[...], g, (((1,), (0,)), ((), ())), preferred_element_type=F32)
            out = out.T.astype(BF16)
            for s in range(8):
                xx, yy = 2 * (s // 4) + k, s % 4
                t[xx + c * (yy - xx), h, yy + c * (xx - yy), zl] = out[s * piece : (s + 1) * piece]
            return carry

        lax.fori_loop(0, 4, body, 0)

    def go(cp):
        cp.start()
        sends.append(cp)

    compute_half(0)
    go(remote(t.at[opp, 0], fwd.at[0], sem_1s.at[0], sem_1r.at[0], dev_r))
    go(remote(t.at[left, 0], own.at[1, 0], sem_1s.at[3], sem_1r.at[3], dev_l))
    compute_half(1)
    go(remote(t.at[opp, 1], fwd.at[1], sem_1s.at[1], sem_1r.at[1], dev_l))
    go(remote(t.at[right, 1], own.at[0, 1], sem_1s.at[2], sem_1r.at[2], dev_r))

    def arrived(dst, ssem, rsem):
        remote(dst, dst, ssem, rsem, partner).wait_recv()

    def add_loop(n, body):
        def step(i, carry):
            body(i)
            return carry

        lax.fori_loop(0, n, step, 0)

    arrived(fwd.at[0], sem_1s.at[0], sem_1r.at[0])

    def add_f0(i):
        b, zl = lax.div(i, 2), lax.rem(i, 2)
        fsum[0, b, zl] = (fwd[0, b, zl].astype(F32) + t[right, 0, b, zl].astype(F32)).astype(BF16)

    add_loop(8, add_f0)
    go(remote(fsum.at[0], own.at[0, 0], sem_1s.at[4], sem_1r.at[4], dev_r))
    arrived(fwd.at[1], sem_1s.at[1], sem_1r.at[1])

    def add_f1(i):
        b, zl = lax.div(i, 2), lax.rem(i, 2)
        fsum[1, b, zl] = (fwd[1, b, zl].astype(F32) + t[left, 1, b, zl].astype(F32)).astype(BF16)

    add_loop(8, add_f1)
    go(remote(fsum.at[1], own.at[1, 1], sem_1s.at[5], sem_1r.at[5], dev_l))

    right2, left2, opp2 = lax.rem(pb_ + 1, 4), lax.rem(pb_ + 3, 4), lax.rem(pb_ + 2, 4)
    dev_r2, dev_l2 = b_dev(1), b_dev(-1)
    arrived(own.at[1, 0], sem_1s.at[3], sem_1r.at[3])
    arrived(own.at[0, 1], sem_1s.at[2], sem_1r.at[2])

    def sum_half(h):
        def body(i):
            b, zl = lax.div(i, 2), lax.rem(i, 2)
            u[h, b, zl] = (
                own[0, h, b, zl].astype(F32) + own[1, h, b, zl].astype(F32) + t[pa, h, b, zl].astype(F32)
            ).astype(BF16)

        add_loop(8, body)

    arrived(own.at[0, 0], sem_1s.at[4], sem_1r.at[4])
    sum_half(0)
    go(remote(u.at[0, opp2], fwd2.at[0], sem_2s.at[0], sem_2r.at[0], dev_r2))
    go(remote(u.at[0, left2], own2.at[1, 0], sem_2s.at[3], sem_2r.at[3], dev_l2))
    arrived(own.at[1, 1], sem_1s.at[5], sem_1r.at[5])
    sum_half(1)
    go(remote(u.at[1, opp2], fwd2.at[1], sem_2s.at[1], sem_2r.at[1], dev_l2))
    go(remote(u.at[1, right2], own2.at[0, 1], sem_2s.at[2], sem_2r.at[2], dev_r2))
    arrived(fwd2.at[0], sem_2s.at[0], sem_2r.at[0])
    fsum2[0] = (fwd2[0].astype(F32) + u[0, right2].astype(F32)).astype(BF16)
    go(remote(fsum2.at[0], own2.at[0, 0], sem_2s.at[4], sem_2r.at[4], dev_r2))
    arrived(fwd2.at[1], sem_2s.at[1], sem_2r.at[1])
    fsum2[1] = (fwd2[1].astype(F32) + u[1, left2].astype(F32)).astype(BF16)
    go(remote(fsum2.at[1], own2.at[1, 1], sem_2s.at[5], sem_2r.at[5], dev_l2))
    arrived(own2.at[1, 0], sem_2s.at[3], sem_2r.at[3])
    arrived(own2.at[0, 1], sem_2s.at[2], sem_2r.at[2])
    arrived(own2.at[0, 0], sem_2s.at[4], sem_2r.at[4])
    w[0] = (own2[0, 0].astype(F32) + own2[1, 0].astype(F32) + u[0, pb_].astype(F32)).astype(BF16)
    arrived(own2.at[1, 1], sem_2s.at[5], sem_2r.at[5])
    w[1] = (own2[0, 1].astype(F32) + own2[1, 1].astype(F32) + u[1, pb_].astype(F32)).astype(BF16)

    for q in range(4):
        dest = 4 * c + q
        src = w.at[q // 2, q % 2]

        @pl.when(z != dest)
        def _():
            remote(src, zr.at[z], sem_zs.at[q], sem_zr.at[z], {"z": dest}).start()

    nz = z - 4 * c
    hz, lz = lax.rem(lax.div(nz + 8, 2), 2), lax.rem(nz + 8, 2)
    quarter = xh

    @pl.when(mine_z)
    def _():
        total = w[hz, lz].astype(F32)
        for d in range(1, 8):
            src_z = lax.rem(z + d, 8)
            arrived(zr.at[src_z], sem_zs.at[0], sem_zr.at[src_z])
            total = total + zr[src_z].astype(F32)
        lr_mine[...] = total

        @pl.when(own_state)
        def _():
            pltpu.make_async_copy(moment.at[m_row], ms.at[0], sem_l.at[4]).wait()
            pltpu.make_async_copy(second.at[m_row], ms.at[1], sem_l.at[5]).wait()

        @pl.when(gets_state)
        def _():
            arrived(ms.at[0], sem_ms.at[0], sem_mr.at[0])
            arrived(ms.at[1], sem_ms.at[1], sem_mr.at[1])

        new_moment, new_second = adam(total, ms[0], ms[1])
        full[c, pa, hz, pb_, lz] = normalize(new_moment, new_second)
        here = full.at[c, pa, hz, pb_, lz]
        for d in range(1, 8):
            remote(here, here, sem_gzs.at[d], sem_gzr.at[nz], {"z": lax.rem(z + d, 8)}).start()

        for dx in range(2):
            for dy in range(4):
                n = dx * 4 + dy
                dev = {"xh": lax.rem(xh + dx, 2), "y": lax.rem(y + dy, 4), "c": quarter}
                cp = remote(lr_mine, lr_out.at[y], sem_ls.at[n], sem_lr.at[y], dev)
                if n == 0:
                    @pl.when(quarter == c)
                    def _():
                        lr_out[y] = total

                    @pl.when(quarter != c)
                    def _():
                        cp.start()
                else:
                    cp.start()

    for q in range(4):
        @pl.when(z != 4 * c + q)
        def _():
            arrived(full.at[c, pa, q // 2, pb_, q % 2], sem_gzs.at[0], sem_gzr.at[q])

    def chunk2(h, b):
        return full.at[c, pa, h, b]

    def hop(ref, ss, rs, i, dev):
        go(remote(ref, ref, ss.at[i], rs.at[i], dev))

    hop(chunk2(0, pb_), sem_bs, sem_br, 0, dev_r2)
    hop(chunk2(1, pb_), sem_bs, sem_br, 1, dev_l2)
    hop(chunk2(1, pb_), sem_bs, sem_br, 2, dev_r2)
    hop(chunk2(0, pb_), sem_bs, sem_br, 3, dev_l2)
    arrived(chunk2(0, left2), sem_bs.at[0], sem_br.at[0])
    hop(chunk2(0, left2), sem_bs, sem_br, 4, dev_r2)
    arrived(chunk2(1, right2), sem_bs.at[1], sem_br.at[1])
    hop(chunk2(1, right2), sem_bs, sem_br, 5, dev_l2)
    arrived(chunk2(1, left2), sem_bs.at[2], sem_br.at[2])
    arrived(chunk2(0, right2), sem_bs.at[3], sem_br.at[3])

    def chunk(h, a):
        return full.at[c, a, h]

    def pass_on(h, a, i):
        go(remote(chunk(h, a), chunk(h, a), sem_ds.at[i], sem_dr.at[i], partner))

    arrived(chunk2(0, opp2), sem_bs.at[4], sem_br.at[4])
    hop(chunk(0, pa), sem_as, sem_ar, 0, dev_r)
    arrived(chunk2(1, opp2), sem_bs.at[5], sem_br.at[5])
    hop(chunk(1, pa), sem_as, sem_ar, 1, dev_l)
    hop(chunk(1, pa), sem_as, sem_ar, 2, dev_r)
    hop(chunk(0, pa), sem_as, sem_ar, 3, dev_l)
    pass_on(0, pa, 0)
    pass_on(1, pa, 1)
    arrived(chunk(0, left), sem_as.at[0], sem_ar.at[0])
    hop(chunk(0, left), sem_as, sem_ar, 4, dev_r)
    pass_on(0, left, 2)
    arrived(chunk(1, right), sem_as.at[1], sem_ar.at[1])
    hop(chunk(1, right), sem_as, sem_ar, 5, dev_l)
    pass_on(1, right, 3)
    arrived(chunk(1, left), sem_as.at[2], sem_ar.at[2])
    pass_on(1, left, 4)
    arrived(chunk(0, right), sem_as.at[3], sem_ar.at[3])
    pass_on(0, right, 5)
    arrived(chunk(0, opp), sem_as.at[4], sem_ar.at[4])
    pass_on(0, opp, 6)
    arrived(chunk(1, opp), sem_as.at[5], sem_ar.at[5])
    pass_on(1, opp, 7)

    for i in range(8):
        arrived(full.at[other, 0, 0], sem_ds.at[i], sem_dr.at[i])
    src_here = lax.div(z, 4) == c
    for q in range(4):
        local = jnp.logical_and(src_here, jnp.logical_and(xh == c, y == q))

        @pl.when(jnp.logical_not(local))
        def _():
            arrived(lr_out.at[q], sem_ls.at[0], sem_lr.at[q])

    for cp in sends:
        cp.wait_send()

    @pl.when(gives_state)
    def _():
        remote(moment.at[m_row], ms.at[0], sem_ms.at[0], sem_mr.at[0], partner).wait_send()
        remote(second.at[m_row], ms.at[1], sem_ms.at[1], sem_mr.at[1], partner).wait_send()

    for q in range(4):
        @pl.when(z != 4 * c + q)
        def _():
            remote(w.at[q // 2, q % 2], zr.at[z], sem_zs.at[q], sem_zr.at[0], partner).wait_send()

    @pl.when(mine_z)
    def _():
        here = full.at[c, pa, hz, pb_, lz]
        for d in range(1, 8):
            remote(here, here, sem_gzs.at[d], sem_gzr.at[0], partner).wait_send()
        for n in range(8):
            cp = remote(lr_mine, lr_out.at[y], sem_ls.at[n], sem_lr.at[0], partner)
            if n == 0:
                @pl.when(quarter != c)
                def _():
                    cp.wait_send()
            else:
                cp.wait_send()


def update_kernel(full, lr, proj, moment, second, update, new_moment, new_second):
    i = pl.program_id(0)
    xl, z = lax.div(i, 8), lax.rem(i, 8)
    c, h, zl = lax.div(z, 4), lax.div(lax.rem(z, 4), 2), lax.rem(z, 2)
    parts = []
    for s in range(8):
        x, y = 2 * (s // 4) + xl, s % 4
        parts.append(full[c, x + c * (y - x), h, y + c * (x - y), zl])
    block = jnp.concatenate(parts, axis=0)
    update[...] = lax.dot_general(
        proj[...], block, (((1,), (1,)), ((), ())), preferred_element_type=F32
    ).astype(BF16)

    @pl.when(i == 0)
    def _():
        m, s = adam(lr[...], moment[...], second[...])
        new_moment[...] = m
        new_second[...] = s


def local(inputs, grad_out, projection, moment, second):
    tok, ff = grad_out.shape
    rank = projection.shape[1]
    piece = ff // 128
    half = (4, 2, piece, rank)
    small = (2, piece, rank)
    anyspace = pl.BlockSpec(memory_space=pl.ANY)
    vmem = pl.BlockSpec(memory_space=pltpu.VMEM)
    dma = pltpu.SemaphoreType.DMA
    full, low_rank = pl.pallas_call(
        comm_kernel,
        out_shape=(
            jax.ShapeDtypeStruct((2, 4, 2) + half, BF16),
            jax.ShapeDtypeStruct((4, piece, rank), F32),
        ),
        in_specs=[anyspace] * 5,
        out_specs=(vmem, vmem),
        scratch_shapes=[
            pltpu.VMEM((2 * tok, 16 * rank), BF16),
            pltpu.VMEM((16 * rank, rank), BF16),
            pltpu.VMEM((2, 2 * tok, ff // 4), BF16),
            pltpu.VMEM((2, 2 * tok, rank), F32),
            pltpu.VMEM((rank, 2 * tok), BF16),
            pltpu.VMEM((2, piece, rank), F32),
            pltpu.VMEM((4, 2) + half, BF16),
            pltpu.VMEM((2,) + half, BF16),
            pltpu.VMEM((2, 2) + half, BF16),
            pltpu.VMEM((2,) + half, BF16),
            pltpu.VMEM((2,) + half, BF16),
            pltpu.VMEM((2,) + small, BF16),
            pltpu.VMEM((2, 2) + small, BF16),
            pltpu.VMEM((2,) + small, BF16),
            pltpu.VMEM((2,) + small, BF16),
            pltpu.VMEM((8, piece, rank), BF16),
            pltpu.VMEM((piece, rank), F32),
            dma((6,)), dma((2,)), dma((16,)), dma((16,)), dma((1,)), dma((1,)), dma((2,)), dma((2,)),
            dma((2,)), dma((2,)),
            dma((6,)), dma((6,)), dma((6,)), dma((6,)), dma((4,)), dma((8,)), dma((8,)), dma((4,)),
            dma((8,)), dma((4,)), dma((6,)), dma((6,)), dma((6,)), dma((6,)), dma((8,)), dma((8,)),
        ],
        compiler_params=pltpu.CompilerParams(
            collective_id=0, has_side_effects=True, vmem_limit_bytes=40 << 20
        ),
        name="exchange",
    )(inputs, grad_out, projection, moment, second)
    low_rank = low_rank.reshape(4 * piece, rank)
    state = pl.BlockSpec((4 * piece, rank), lambda i: (0, 0))
    return pl.pallas_call(
        update_kernel,
        grid=(16,),
        out_shape=(
            jax.ShapeDtypeStruct((rank, ff), BF16),
            jax.ShapeDtypeStruct(moment.shape, F32),
            jax.ShapeDtypeStruct(second.shape, F32),
        ),
        in_specs=[
            pl.BlockSpec((2, 4, 2) + half, lambda i: (0,) * 7),
            state,
            pl.BlockSpec((rank, rank), lambda i: (0, 0)),
            state,
            state,
        ],
        out_specs=(pl.BlockSpec((rank, 8 * piece), lambda i: (0, i)), state, state),
        compiler_params=pltpu.CompilerParams(vmem_limit_bytes=20 << 20),
        name="update",
    )(full, low_rank, projection, moment, second)


def solution(mesh):
    split = Mesh(mesh.devices.reshape(2, 8, 2, 4, 2), AXES)
    return jax.shard_map(
        local,
        mesh=split,
        in_specs=(P(AXES, None), P(AXES, None), P(FSDP, None), P(FSDP, None), P(FSDP, None)),
        out_specs=(P(FSDP, None), P(FSDP, None), P(FSDP, None)),
        check_vma=False,
    )
```

time: 278 us -> 97.6 us (0.35)
  waiting for transfers between devices: 165 us -> 0 us
  Pallas kernels: 0 us -> 90.1 us
  blocking collectives: 59.6 us -> 0 us
  local copies, waits for them, and re-layouts: 23.8 us -> 6.59 us
  between operations: 13.8 us -> 0.65 us
  matrix products: 12.3 us -> 0 us
  other arithmetic: 2.82 us -> 0 us
    reduce_scatter x2 -> x0, waiting for transfers between devices: 95 us -> none  [the longest x1 73.8 us: scatter_pairs(): return lax.psum_scatter(parts, chips, scatter_dimension=0, tiled=True)[0]]
    pallas_call x0 -> x2, Pallas kernels: none -> 90.1 us  [the longest x1 82.2 us: local(): pl.pallas_call(comm_kernel, out_shape=(jax.ShapeDtypeStruct((2, 4, 2) + h...]
    all_gather x1 -> x0, waiting for transfers between devices: 70 us -> none  [local(): lax.all_gather(normalized, FSDP, axis=0, tiled=True)]
    all_to_all x2 -> x0, blocking collectives: 59.6 us -> none  [copy_for_each(): return lax.all_to_all(copies, axis, split_axis=0, concat_axis=0, tiled=True)]
    dot_general x2 -> x0, matrix products: 12.3 us -> none  [the longest x1 7.29 us: local(): lax.dot_general(grad_out, projected, contract, preferred_element_type=jnp...]
    dot_general x1 -> x0, local copies, waits for them, and re-layouts: 8.64 us -> none  [local(): lax.dot_general(grad_out, projected, contract, preferred_element_type=jnp...]
    transpose x1 -> x0, local copies, waits for them, and re-layouts: 6.88 us -> none  [scatter_pairs(): parts = parts.reshape(*sizes, *inside).swapaxes(0, 1).reshape(-1, *inside)]
    unnamed x5 -> x10, local copies, waits for them, and re-layouts: 6.09 us -> 6.59 us
  transfers between devices with their start and end apart: 3 -> 0, of which waited for: 3 -> 0; matrix products, arithmetic and copies ran while one was open for 0% -> 0% of each run, Pallas kernels for 0% -> 0%
where the time goes in v1:
time: 97.6 us; the launch traced here: 97.3 us
  Pallas kernels  90.1 us (92%)
  local copies, waits for them, and re-layouts  6.59 us (7%)
    pallas_call x1, Pallas kernels, local(): pl.pallas_call(comm_kernel, out_shape=(jax.ShapeDtypeStruct((2, 4, 2) + h...  82.2 us
    pallas_call x1, Pallas kernels, local(): pl.pallas_call(update_kernel, grid=(16,), out_shape=(jax.ShapeDtypeStruct...  7.91 us
    unnamed x10, local copies, waits for them, and re-layouts  6.59 us

profile of v1, /device:TPU:1, one launch (start us, length us, event | category | flops | bytes accessed | tf_op | source)
XLA Modules:
  0.0 97.3 jit_solution(8754667764557636692)
XLA Ops:
  0.6 0.0 copy-start
  0.6 2.6 %copy-done = bf16[192,14336]{1,0:T(8,128)(2,1)S(1)} copy-done((bf16[192,14336]{1,0:T(8,128)(2,1)S(1)}, bf16[192,14336]{1,0:T(8,128)(2,1)}, u32[]{:S(2)}) %copy-start) | copy-done | bytes 5505048
  3.2 0.0 copy-start.1
  3.2 1.4 %copy-done.1 = bf16[192,4096]{1,0:T(8,128)(2,1)S(1)} copy-done((bf16[192,4096]{1,0:T(8,128)(2,1)S(1)}, bf16[192,4096]{1,0:T(8,128)(2,1)}, u32[]{:S(2)}) %copy-start.1) | copy-done | bytes 1572888
  4.6 0.0 copy-start.2
  4.6 0.9 copy-done.2
  5.5 0.0 copy-start.3
  5.5 0.9 copy-done.3
  6.5 0.0 copy-start.4
  6.5 0.8 copy-done.4
  7.2 82.2 %exchange.1 = (bf16[2,4,2,4,2,112,128]{6,5,4,3,2,1,0:T(8,128)(2,1)S(1)}, f32[4,112,128]{2,1,0:T(8,128)S(1)}) custom-call(bf16[192,4096]{1,0:T(8,128)(2,1)S(1)} %copy-done.1, bf16[192,14336]{1,0:T(8,128)(2,1)S(1)} %copy-done, bf16[128,128]{1,0:T(8,128)(2,1)S(1)} %copy-done.4, f32[448,128]{1,0:T(8,128)S(1)} %copy-done.2, f32[448,128]{1,0:T(8,128)S(1)} %copy-done.3), custom_call_target="tpu_custom_call" | custom-call | tf_op jit(solution)/shard_map/exchange/pallas_call | solution.py:424
  89.4 7.9 %update.1 = (bf16[128,14336]{1,0:T(8,128)(2,1)}, f32[448,128]{1,0:T(8,128)}, f32[448,128]{1,0:T(8,128)}) custom-call(bf16[2,4,2,4,2,112,128]{6,5,4,3,2,1,0:T(8,128)(2,1)S(1)} %get-tuple-element.5.full, f32[448,128]{1,0:T(8,128)S(1)} %bitcast.1, bf16[128,128]{1,0:T(8,128)(2,1)S(1)} %copy-done.4, f32[448,128]{1,0:T(8,128)S(1)} %copy-done.2, ...), custom_call_target="tpu_custom_call" | custom-call | tf_op jit(solution)/shard_map/update/pallas_call | solution.py:462
Async XLA Ops:
  0.6 2.6 %copy-start = (bf16[192,14336]{1,0:T(8,128)(2,1)S(1)}, bf16[192,14336]{1,0:T(8,128)(2,1)}, u32[]{:S(2)}) copy-start(bf16[192,14336]{1,0:T(8,128)(2,1)} %grad.1) | copy-start | bytes 16515076
  3.2 1.4 %copy-start.1 = (bf16[192,4096]{1,0:T(8,128)(2,1)S(1)}, bf16[192,4096]{1,0:T(8,128)(2,1)}, u32[]{:S(2)}) copy-start(bf16[192,4096]{1,0:T(8,128)(2,1)} %inputs.1) | copy-start | bytes 4718596
  4.6 0.9 copy-start.2
  5.5 0.9 copy-start.3
  6.5 0.8 copy-start.4
